TPU v7x, 32 devices: a whole 2x2x4 slice. The times are simulated.
32 devices in a mesh: parts: 2 (over y), slab: 4 (over z), valley: 2 (over x), blk: 2 (over core).
Axes of the slice: x: 2, y: 2, z: 4, core: 2. Of those that a mesh axis runs over, the one named last changes fastest.
Arguments:
- potential: bfloat16 [64, 2048], P('slab'), may hold values from -3.5 to 4
- mode_density: bfloat16 [4, 2048, 2048], P(('parts', 'valley'), 'blk'), parts along dimension 0, may hold values from 0 to 1, as said below
- energy: float32 [4], P(('parts', 'valley')), parts along dimension 0, may hold values from -0.5 to 0.5
- hopping: float32 [4], P(('parts', 'valley')), parts along dimension 0, may hold values from 0.6 to 1.4
- mode_energy: float32 [4, 2048], P(('parts', 'valley'), 'blk'), parts along dimension 0, may hold values from -2.5 to 3
- broadening: float32 [4, 2048], P(('parts', 'valley'), 'blk'), parts along dimension 0, may hold values from 0.0078125 to 0.3
- self_left: float32 [4, 2, 2048], P(('parts', 'valley'), None, 'blk'), parts along dimension 0, may hold values from -1 to 1, as said below
- self_right: float32 [4, 2, 2048], P(('parts', 'valley'), None, 'blk'), parts along dimension 0, may hold values from -1 to 1, as said below
- occupation: float32 [4], P(('parts', 'valley')), parts along dimension 0, may hold values from 0.5 to 1.5
Outputs:
- mode_charge: float32 [4, 64, 2048], P(('parts', 'valley'), 'slab', 'blk'), parts along dimension 0
- electron_density: float32 [128, 2048], P(('parts', 'slab'), ('valley', 'blk')), parts along dimension 0
There are 2 independent parts, one for each index of `parts`. A program takes and returns all parts, laid end to end along the dimension named above; an argument that names none is the same for every part. Nothing has to cross between parts.
Inputs may be any that keep to these rules, and one draw needn't show every extreme that they name: `mode_density`: every entry is positive. `self_left`: the imaginary parts (index 1 of the second dimension) are negative. `self_right`: the imaginary parts (index 1 of the second dimension) are negative.
All inputs are finite; a program needn't handle non-finite values.
Results may differ from a plain program's by a relative error of at most 0.0065.
Values sent between devices are 32-bit elements; how exact they have to be, the bound alone decides.
A program may use at most 64 MiB of HBM per device.

v0:
```python
import functools
import math

import jax
import jax.numpy as jnp
from jax import lax
from jax.experimental import pallas as pl
from jax.experimental.pallas import tpu as pltpu
from jax.sharding import PartitionSpec as P

MESH = pl.DeviceIdType.MESH
LANES = 128
CHUNKS = 2


def times(x, y):
    return x[0] * y[0] - x[1] * y[1], x[0] * y[1] + x[1] * y[0]


def inverse(x):
    scale = 1.0 / (x[0] * x[0] + x[1] * x[1])
    return x[0] * scale, -(x[1] * scale)


def through(near, cross, far, hop_square, term):
    turn = times(near, term)
    share = times(times(cross, term), inverse((1.0 - turn[0], -turn[1])))
    return hop_square * (far[0] + share[0]), hop_square * (far[1] + share[1])


def kernel(
    sizes,
    potential_at,
    mode_density,
    energy,
    hopping,
    mode_energy_at,
    broadening_at,
    self_left_at,
    self_right_at,
    occupation,
    charge_out,
    density_out,
    profile,
    potential,
    mode_energy,
    broadening,
    self_left,
    self_right,
    folded,
    small,
    terms,
    heads,
    tails,
    own,
    others,
    parts_own,
    parts_in,
    load_sem,
    small_sem,
    send_sem,
    recv_sem,
    send2_sem,
    recv2_sem,
):
    groups, valleys, blks = sizes
    slabs = potential.shape[0]
    modes, width = profile.shape
    rows = modes // LANES
    team = valleys * blks
    columns = width // team
    me = lax.axis_index("slab")
    valley = lax.axis_index("valley")
    blk = lax.axis_index("blk")

    small_loads = []
    for slot, (source, target) in enumerate(
        [
            (potential_at, potential),
            (mode_energy_at, mode_energy),
            (broadening_at, broadening),
            (self_left_at, self_left),
            (self_right_at, self_right),
        ]
    ):
        load = pltpu.make_async_copy(source, target, small_sem.at[slot])
        load.start()
        small_loads.append(load)
    size = modes // CHUNKS
    loads = []
    for q in range(CHUNKS):
        span = pl.ds(q * size, size)
        load = pltpu.make_async_copy(
            mode_density.at[0, span, :], profile.at[span, :], load_sem.at[q]
        )
        load.start()
        loads.append(load)

    offsets = [(dv, db) for dv in range(1, valleys) for db in range(blks)]
    offsets += [(0, db) for db in range(1, blks)]
    mates = [(lax.rem(valley + dv, valleys), lax.rem(blk + db, blks)) for dv, db in offsets]
    barrier = pltpu.get_barrier_semaphore()
    for d in range(1, groups):
        pl.semaphore_signal(
            barrier, inc=1, device_id={"slab": lax.rem(me + d, groups)}, device_id_type=MESH
        )
    for tv, tb in mates:
        pl.semaphore_signal(
            barrier, inc=1, device_id={"valley": tv, "blk": tb}, device_id_type=MESH
        )

    for load in small_loads:
        load.wait()
    hop_square = hopping[0] * hopping[0]
    for j in range(rows):
        span = pl.ds(j * LANES, LANES)
        small[0, pl.ds(j, 1), :] = energy[0] - mode_energy[:, span]
        small[1, pl.ds(j, 1), :] = broadening[:, span]
        for part in range(2):
            small[2 + part, pl.ds(j, 1), :] = self_left[0, pl.ds(part, 1), span]
            small[4 + part, pl.ds(j, 1), :] = self_right[0, pl.ds(part, 1), span]

    for q in range(CHUNKS):
        loads[q].wait()
        projected = lax.dot_general(
            potential[...],
            profile[pl.ds(q * size, size), :],
            (((1,), (1,)), ((), ())),
            preferred_element_type=jnp.float32,
        )
        for j in range(size // LANES):
            row = q * (size // LANES) + j
            folded[pl.ds(row, slabs, stride=rows), :] = projected[:, j * LANES : (j + 1) * LANES]

    level = small[0]
    onsite_im = small[1]

    def onsite(s):
        return level - folded[pl.ds(s * rows, rows), :], onsite_im

    def start(s):
        far = inverse(onsite(s))
        return far, times(far, far), far

    def grow(segment, s):
        near, cross, far = segment
        site = onsite(s)
        far = inverse((site[0] - hop_square * far[0], site[1] - hop_square * far[1]))
        linked = times(cross, far)
        linked = hop_square * linked[0], hop_square * linked[1]
        return (near[0] + linked[0], near[1] + linked[1]), times(linked, far), far

    def merge(one, two):
        turn = times(one[2], two[0])
        back = inverse((1.0 - hop_square * turn[0], -(hop_square * turn[1])))
        back = hop_square * back[0], hop_square * back[1]
        more_near = times(times(one[1], two[0]), back)
        more_far = times(times(two[1], one[2]), back)
        near = one[0][0] + more_near[0], one[0][1] + more_near[1]
        far = two[2][0] + more_far[0], two[2][1] + more_far[1]
        cross = times(times(one[1], back), times(two[1], back))
        scale = 1.0 / hop_square
        return near, (scale * cross[0], scale * cross[1]), far

    pieces = []
    run = 4 if slabs % 4 == 0 else slabs
    for first in range(0, slabs, run):
        piece = start(first)
        for s in range(first + 1, first + run):
            piece = grow(piece, s)
        pieces.append(piece)
    while len(pieces) > 1:
        pairs = [merge(x, y) for x, y in zip(pieces[0::2], pieces[1::2])]
        pieces = pairs + pieces[2 * len(pairs) :]
    near, cross, far = pieces[0]
    begin, end = (small[2], small[3]), (small[4], small[5])
    after = through(near, cross, far, hop_square, begin)
    before = through(far, cross, near, hop_square, end)
    is_first, is_last = me == 0, me == groups - 1
    for part in range(2):
        own[part] = jnp.where(is_first, after[part], jnp.where(is_last, before[part], near[part]))
        own[2 + part] = cross[part]
        own[4 + part] = far[part]
        others[0, part] = jnp.where(is_first, begin[part], end[part])

    pl.semaphore_wait(barrier, groups - 1 + team - 1)
    inner = jnp.logical_and(me > 0, me < groups - 1)
    planes = (pl.ds(0, 2), pl.ds(2, 4))
    routes = []
    for distance in range(groups - 1, 0, -1):
        routes.append((me + distance, me - distance, distance))
        routes.append((me - distance, me + distance, groups - distance))
    sends = []
    for target, source, slot in routes:
        copies = [
            pltpu.make_async_remote_copy(
                src_ref=own.at[plane],
                dst_ref=others.at[slot, plane],
                send_sem=send_sem.at[slot, which],
                recv_sem=recv_sem.at[slot, which],
                device_id={"slab": lax.rem(target + groups, groups)},
                device_id_type=MESH,
            )
            for which, plane in enumerate(planes)
        ]
        going = jnp.logical_and(target >= 0, target < groups)
        coming = jnp.logical_and(source >= 0, source < groups)
        full = jnp.logical_and(source > 0, source < groups - 1)
        sends.append((copies, going, coming, full))
    for copies, going, coming, full in sends:

        @pl.when(going)
        def _():
            copies[0].start()

        @pl.when(jnp.logical_and(going, inner))
        def _():
            copies[1].start()

    segment = start(0)
    for s in range(slabs - 1):
        for part in range(6):
            heads[s, part] = segment[part // 2][part % 2]
        if s + 1 < slabs - 1:
            segment = grow(segment, s + 1)
    segment = start(slabs - 1)
    for s in range(slabs - 1, 0, -1):
        for part in range(6):
            tails[s - 1, part] = segment[part // 2][part % 2]
        if s > 1:
            segment = grow(segment, s - 1)

    for copies, going, coming, full in sends:

        @pl.when(coming)
        def _():
            copies[0].wait_recv()

        @pl.when(full)
        def _():
            copies[1].wait_recv()

    def corners(ref, index):
        values = [ref[index, part] for part in range(6)]
        return values[0:2], values[2:4], values[4:6]

    def go_right(k, term):
        near, cross, far = corners(others, me - k)
        return through(near, cross, far, hop_square, term)

    def go_left(step, term):
        near, cross, far = corners(others, step)
        return through(far, cross, near, hop_square, term)

    if groups == 1:
        left, right = begin, end
    else:
        edge = lax.rem(me + 1, groups)
        left = lax.fori_loop(1, me, go_right, (others[me, 0], others[me, 1]))
        right = lax.fori_loop(me + 2, groups, go_left, (others[edge, 0], others[edge, 1]))

    factor = occupation[0] * (1.0 / math.pi)
    for s in range(slabs):
        site = onsite(s)
        a, b = left, right
        if s > 0:
            near, cross, far = corners(heads, s - 1)
            a = through(near, cross, far, hop_square, left)
        if s < slabs - 1:
            near, cross, far = corners(tails, s)
            b = through(near, cross, far, hop_square, right)
        low_re = site[0] - a[0] - b[0]
        low_im = site[1] - a[1] - b[1]
        terms[pl.ds(s * rows, rows), :] = factor * low_im / (low_re * low_re + low_im * low_im)

    for j in range(rows):
        charge_out[0, :, pl.ds(j * LANES, LANES)] = terms[pl.ds(j, slabs, stride=rows), :]
    half = charge_out[0].astype(jnp.bfloat16)

    def share(owner):
        span = pl.ds(pl.multiple_of(owner * columns, columns), columns)
        return jnp.dot(half, profile[:, span], preferred_element_type=jnp.float32)

    sends2 = []
    for slot, (tv, tb) in enumerate(mates):
        parts_own[slot] = share(tv * blks + tb)
        send = pltpu.make_async_remote_copy(
            src_ref=parts_own.at[slot],
            dst_ref=parts_in.at[slot],
            send_sem=send2_sem.at[slot],
            recv_sem=recv2_sem.at[slot],
            device_id={"valley": tv, "blk": tb},
            device_id_type=MESH,
        )
        send.start()
        sends2.append(send)
    total = share(valley * blks + blk)
    for slot in reversed(range(len(mates))):
        sends2[slot].wait_recv()
        total = total + parts_in[slot]
    density_out[...] = total
    for send in sends2:
        send.wait_send()
    for copies, going, coming, full in sends:

        @pl.when(going)
        def _():
            copies[0].wait_send()

        @pl.when(jnp.logical_and(going, inner))
        def _():
            copies[1].wait_send()


def drain(charge, density, charge_out, density_out, sem):
    first = pltpu.make_async_copy(charge, charge_out, sem.at[0])
    second = pltpu.make_async_copy(density, density_out, sem.at[1])
    first.start()
    second.start()
    first.wait()
    second.wait()


def solution(mesh):
    sizes = (mesh.shape["slab"], mesh.shape["valley"], mesh.shape["blk"])
    groups, valleys, blks = sizes
    team = valleys * blks

    def body(potential, mode_density, *rest):
        slabs = potential.shape[0]
        modes, width = mode_density.shape[1:]
        rows = modes // LANES
        columns = width // team
        vmem = pl.BlockSpec(memory_space=pltpu.VMEM)
        smem = pl.BlockSpec(memory_space=pltpu.SMEM)
        hbm = pl.BlockSpec(memory_space=pltpu.HBM)
        operands = [
            x if x.ndim == 1 else pltpu.with_memory_space_constraint(x, pltpu.HBM)
            for x in (potential, mode_density, *rest)
        ]
        outs = pl.pallas_call(
            functools.partial(kernel, sizes),
            out_shape=(
                pltpu.VMEM((1, slabs, modes), jnp.float32),
                pltpu.VMEM((slabs, columns), jnp.float32),
            ),
            in_specs=[hbm, hbm, smem, smem, hbm, hbm, hbm, hbm, smem],
            out_specs=(vmem, vmem),
            scratch_shapes=[
                pltpu.VMEM((modes, width), jnp.bfloat16),
                pltpu.VMEM((slabs, width), jnp.bfloat16),
                pltpu.VMEM((1, modes), jnp.float32),
                pltpu.VMEM((1, modes), jnp.float32),
                pltpu.VMEM((1, 2, modes), jnp.float32),
                pltpu.VMEM((1, 2, modes), jnp.float32),
                pltpu.VMEM((slabs * rows, LANES), jnp.float32),
                pltpu.VMEM((6, rows, LANES), jnp.float32),
                pltpu.VMEM((slabs * rows, LANES), jnp.float32),
                pltpu.VMEM((max(slabs - 1, 1), 6, rows, LANES), jnp.float32),
                pltpu.VMEM((max(slabs - 1, 1), 6, rows, LANES), jnp.float32),
                pltpu.VMEM((6, rows, LANES), jnp.float32),
                pltpu.VMEM((groups, 6, rows, LANES), jnp.float32),
                pltpu.VMEM((max(team - 1, 1), slabs, columns), jnp.float32),
                pltpu.VMEM((max(team - 1, 1), slabs, columns), jnp.float32),
                pltpu.SemaphoreType.DMA((CHUNKS,)),
                pltpu.SemaphoreType.DMA((5,)),
                pltpu.SemaphoreType.DMA((groups, 2)),
                pltpu.SemaphoreType.DMA((groups, 2)),
                pltpu.SemaphoreType.DMA((max(team - 1, 1),)),
                pltpu.SemaphoreType.DMA((max(team - 1, 1),)),
            ],
            compiler_params=pltpu.CompilerParams(
                collective_id=0, has_side_effects=True, vmem_limit_bytes=16 * 1024 * 1024
            ),
        )(*operands)

        return pl.pallas_call(
            drain,
            out_shape=(
                jax.ShapeDtypeStruct((1, slabs, modes), jnp.float32),
                jax.ShapeDtypeStruct((slabs, columns), jnp.float32),
            ),
            in_specs=[vmem, vmem],
            out_specs=(hbm, hbm),
            scratch_shapes=[pltpu.SemaphoreType.DMA((2,))],
            compiler_params=pltpu.CompilerParams(vmem_limit_bytes=1024 * 1024),
        )(*outs)

    placed = (
        P("slab", None),
        P(("parts", "valley"), "blk", None),
        P(("parts", "valley")),
        P(("parts", "valley")),
        P(("parts", "valley"), "blk"),
        P(("parts", "valley"), "blk"),
        P(("parts", "valley"), None, "blk"),
        P(("parts", "valley"), None, "blk"),
        P(("parts", "valley")),
    )
    return jax.shard_map(
        body,
        mesh=mesh,
        in_specs=placed,
        out_specs=(P(("parts", "valley"), "slab", "blk"), P(("parts", "slab"), ("valley", "blk"))),
        check_vma=False,
    )
```

profile of v0, /device:TPU:0, one launch (start us, length us, event | category | flops | bytes accessed | tf_op | source)
XLA Modules:
  0.0 17.2 jit_solution(11640902465469520858)
XLA Ops:
  2.6 14.0 %shard_map.104 = (f32[1,16,1024]{2,1,0:T(8,128)S(1)}, f32[16,512]{1,0:T(8,128)S(1)}) custom-call(bf16[16,2048]{1,0:T(8,128)(2,1)} %potential_at.1, bf16[1,1024,2048]{2,1,0:T(8,128)(2,1)} %mode_density.1, f32[1]{0:T(128)S(6)} %copy.11.energy, f32[1]{0:T(128)S(6)} %copy.12.hopping, f32[1,1024]{1,0:T(1,128)} %mode_energy_at.1, f32[1,1024]{1,0:T(1,128)} %broadening_at.1, ...), custom_call_target="tpu_custom_call" | custom-call | tf_op jit(solution)/shard_map/pallas_call | solution.py:341
  16.5 0.7 %shard_map.105 = (f32[1,16,1024]{2,1,0:T(8,128)}, f32[16,512]{1,0:T(8,128)}) custom-call(f32[1,16,1024]{2,1,0:T(8,128)S(1)} %get-tuple-element.4.charge, f32[16,512]{1,0:T(8,128)S(1)} %get-tuple-element.5.density), custom_call_target="tpu_custom_call" | custom-call | tf_op jit(solution)/shard_map/pallas_call | solution.py:377
where the time goes:
time: 17.4 us; the launch traced here: 17.2 us
  Pallas kernels  14.6 us (84%)
  between operations  2.58 us (15%)
    pallas_call x1, Pallas kernels, body(): pl.pallas_call(functools.partial(kernel, sizes), out_shape=(pltpu.VMEM((1...  14 us
    pallas_call x1, Pallas kernels, body(): pl.pallas_call(drain, out_shape=(jax.ShapeDtypeStruct((1, slabs, modes),...  0.66 us

commit v1 on v0

--- a/solution.py
+++ b/solution.py
@@ -10,7 +10,7 @@
 
 MESH = pl.DeviceIdType.MESH
 LANES = 128
-CHUNKS = 2
+PIECE = 256
 
 
 def times(x, y):
@@ -28,21 +28,24 @@
     return hop_square * (far[0] + share[0]), hop_square * (far[1] + share[1])
 
 
+def spread(energy, hopping, occupation, scalars):
+    shape = scalars.shape[1:]
+    scalars[0] = jnp.full(shape, energy[0])
+    scalars[1] = jnp.full(shape, hopping[0] * hopping[0])
+    scalars[2] = jnp.full(shape, occupation[0] * (1.0 / math.pi))
+
+
 def kernel(
     sizes,
-    potential_at,
-    mode_density,
-    energy,
-    hopping,
+    potential,
+    profile_at,
+    scalars,
     mode_energy_at,
     broadening_at,
     self_left_at,
     self_right_at,
-    occupation,
     charge_out,
     density_out,
-    profile,
-    potential,
     mode_energy,
     broadening,
     self_left,
@@ -56,15 +59,15 @@
     others,
     parts_own,
     parts_in,
-    load_sem,
-    small_sem,
     send_sem,
     recv_sem,
     send2_sem,
     recv2_sem,
+    small_sem,
 ):
     groups, valleys, blks = sizes
     slabs = potential.shape[0]
+    profile = profile_at.at[0]
     modes, width = profile.shape
     rows = modes // LANES
     team = valleys * blks
@@ -73,28 +76,19 @@
     valley = lax.axis_index("valley")
     blk = lax.axis_index("blk")
 
-    small_loads = []
-    for slot, (source, target) in enumerate(
-        [
-            (potential_at, potential),
-            (mode_energy_at, mode_energy),
-            (broadening_at, broadening),
-            (self_left_at, self_left),
-            (self_right_at, self_right),
-        ]
-    ):
-        load = pltpu.make_async_copy(source, target, small_sem.at[slot])
+    small_loads = [
+        pltpu.make_async_copy(source, target, small_sem.at[slot])
+        for slot, (source, target) in enumerate(
+            [
+                (mode_energy_at, mode_energy),
+                (broadening_at, broadening),
+                (self_left_at, self_left),
+                (self_right_at, self_right),
+            ]
+        )
+    ]
+    for load in small_loads:
         load.start()
-        small_loads.append(load)
-    size = modes // CHUNKS
-    loads = []
-    for q in range(CHUNKS):
-        span = pl.ds(q * size, size)
-        load = pltpu.make_async_copy(
-            mode_density.at[0, span, :], profile.at[span, :], load_sem.at[q]
-        )
-        load.start()
-        loads.append(load)
 
     offsets = [(dv, db) for dv in range(1, valleys) for db in range(blks)]
     offsets += [(0, db) for db in range(1, blks)]
@@ -109,28 +103,28 @@
             barrier, inc=1, device_id={"valley": tv, "blk": tb}, device_id_type=MESH
         )
 
+    size = math.gcd(modes, PIECE)
+    for first in range(0, modes, size):
+        projected = lax.dot_general(
+            potential[...],
+            profile[pl.ds(first, size), :],
+            (((1,), (1,)), ((), ())),
+            preferred_element_type=jnp.float32,
+        )
+        for j in range(size // LANES):
+            row = first // LANES + j
+            folded[pl.ds(row, slabs, stride=rows), :] = projected[:, j * LANES : (j + 1) * LANES]
+
     for load in small_loads:
         load.wait()
-    hop_square = hopping[0] * hopping[0]
+    hop_square = scalars[1]
     for j in range(rows):
         span = pl.ds(j * LANES, LANES)
-        small[0, pl.ds(j, 1), :] = energy[0] - mode_energy[:, span]
+        small[0, pl.ds(j, 1), :] = scalars[0, pl.ds(j, 1), :] - mode_energy[:, span]
         small[1, pl.ds(j, 1), :] = broadening[:, span]
         for part in range(2):
             small[2 + part, pl.ds(j, 1), :] = self_left[0, pl.ds(part, 1), span]
             small[4 + part, pl.ds(j, 1), :] = self_right[0, pl.ds(part, 1), span]
-
-    for q in range(CHUNKS):
-        loads[q].wait()
-        projected = lax.dot_general(
-            potential[...],
-            profile[pl.ds(q * size, size), :],
-            (((1,), (1,)), ((), ())),
-            preferred_element_type=jnp.float32,
-        )
-        for j in range(size // LANES):
-            row = q * (size // LANES) + j
-            folded[pl.ds(row, slabs, stride=rows), :] = projected[:, j * LANES : (j + 1) * LANES]
 
     level = small[0]
     onsite_im = small[1]
@@ -259,7 +253,7 @@
         left = lax.fori_loop(1, me, go_right, (others[me, 0], others[me, 1]))
         right = lax.fori_loop(me + 2, groups, go_left, (others[edge, 0], others[edge, 1]))
 
-    factor = occupation[0] * (1.0 / math.pi)
+    factor = scalars[2]
     for s in range(slabs):
         site = onsite(s)
         a, b = left, right
@@ -326,7 +320,17 @@
     groups, valleys, blks = sizes
     team = valleys * blks
 
-    def body(potential, mode_density, *rest):
+    def body(
+        potential,
+        mode_density,
+        energy,
+        hopping,
+        mode_energy,
+        broadening,
+        self_left,
+        self_right,
+        occupation,
+    ):
         slabs = potential.shape[0]
         modes, width = mode_density.shape[1:]
         rows = modes // LANES
@@ -334,9 +338,19 @@
         vmem = pl.BlockSpec(memory_space=pltpu.VMEM)
         smem = pl.BlockSpec(memory_space=pltpu.SMEM)
         hbm = pl.BlockSpec(memory_space=pltpu.HBM)
-        operands = [
-            x if x.ndim == 1 else pltpu.with_memory_space_constraint(x, pltpu.HBM)
-            for x in (potential, mode_density, *rest)
+        scalars = pl.pallas_call(
+            spread,
+            out_shape=pltpu.VMEM((3, rows, LANES), jnp.float32),
+            in_specs=[smem] * 3,
+            out_specs=vmem,
+            cost_estimate=pl.CostEstimate(
+                flops=1_600_000_000, bytes_accessed=1 << 16, transcendentals=0
+            ),
+            compiler_params=pltpu.CompilerParams(vmem_limit_bytes=1024 * 1024),
+        )(energy, hopping, occupation)
+        smalls = [
+            pltpu.with_memory_space_constraint(x, pltpu.HBM)
+            for x in (mode_energy, broadening, self_left, self_right)
         ]
         outs = pl.pallas_call(
             functools.partial(kernel, sizes),
@@ -344,11 +358,9 @@
                 pltpu.VMEM((1, slabs, modes), jnp.float32),
                 pltpu.VMEM((slabs, columns), jnp.float32),
             ),
-            in_specs=[hbm, hbm, smem, smem, hbm, hbm, hbm, hbm, smem],
+            in_specs=[vmem, vmem, vmem, hbm, hbm, hbm, hbm],
             out_specs=(vmem, vmem),
             scratch_shapes=[
-                pltpu.VMEM((modes, width), jnp.bfloat16),
-                pltpu.VMEM((slabs, width), jnp.bfloat16),
                 pltpu.VMEM((1, modes), jnp.float32),
                 pltpu.VMEM((1, modes), jnp.float32),
                 pltpu.VMEM((1, 2, modes), jnp.float32),
@@ -362,17 +374,16 @@
                 pltpu.VMEM((groups, 6, rows, LANES), jnp.float32),
                 pltpu.VMEM((max(team - 1, 1), slabs, columns), jnp.float32),
                 pltpu.VMEM((max(team - 1, 1), slabs, columns), jnp.float32),
-                pltpu.SemaphoreType.DMA((CHUNKS,)),
-                pltpu.SemaphoreType.DMA((5,)),
                 pltpu.SemaphoreType.DMA((groups, 2)),
                 pltpu.SemaphoreType.DMA((groups, 2)),
                 pltpu.SemaphoreType.DMA((max(team - 1, 1),)),
                 pltpu.SemaphoreType.DMA((max(team - 1, 1),)),
+                pltpu.SemaphoreType.DMA((4,)),
             ],
             compiler_params=pltpu.CompilerParams(
-                collective_id=0, has_side_effects=True, vmem_limit_bytes=16 * 1024 * 1024
+                collective_id=0, has_side_effects=True, vmem_limit_bytes=8 * 1024 * 1024
             ),
-        )(*operands)
+        )(potential, mode_density, scalars, *smalls)
 
         return pl.pallas_call(
             drain,

time: 17.4 us -> 16.3 us (0.937)
  Pallas kernels: 14.6 us -> 12.9 us
  between operations: 2.58 us -> 3.17 us
    pallas_call x1, Pallas kernels: 14 us -> 12.3 us  [body(): pl.pallas_call(functools.partial(kernel, sizes), out_shape=(pltpu.VMEM((1...]
where the time goes in v1:
time: 16.3 us; the launch traced here: 16.1 us
  Pallas kernels  12.9 us (79%)
  between operations  3.17 us (19%)
    pallas_call x1, Pallas kernels, body(): pl.pallas_call(functools.partial(kernel, sizes), out_shape=(pltpu.VMEM((1...  12.3 us
    pallas_call x1, Pallas kernels, body(): pl.pallas_call(drain, out_shape=(jax.ShapeDtypeStruct((1, slabs, modes),...  0.66 us

profile of v1, /device:TPU:0, one launch (start us, length us, event | category | flops | bytes accessed | tf_op | source)
XLA Modules:
  0.0 16.1 jit_solution(11462333639828068491)
XLA Ops:
  0.6 0.0 copy-start
  0.6 0.0 copy-start.1
  3.2 0.0 copy-done
  3.2 0.0 copy-done.1
  3.2 12.3 %shard_map.105 = (f32[1,16,1024]{2,1,0:T(8,128)S(1)}, f32[16,512]{1,0:T(8,128)S(1)}) custom-call(bf16[16,2048]{1,0:T(8,128)(2,1)S(1)} %copy-done.1, bf16[1,1024,2048]{2,1,0:T(8,128)(2,1)S(1)} %copy-done, f32[3,8,128]{2,1,0:T(8,128)S(1)} %shard_map.104.scalars, f32[1,1024]{1,0:T(1,128)} %mode_energy_at.1, f32[1,1024]{1,0:T(1,128)} %broadening_at.1, ...), custom_call_target="tpu_custom_call" | custom-call | tf_op jit(solution)/shard_map/pallas_call | solution.py:355
  15.4 0.7 %shard_map.106 = (f32[1,16,1024]{2,1,0:T(8,128)}, f32[16,512]{1,0:T(8,128)}) custom-call(f32[1,16,1024]{2,1,0:T(8,128)S(1)} %get-tuple-element.4.charge, f32[16,512]{1,0:T(8,128)S(1)} %get-tuple-element.5.density), custom_call_target="tpu_custom_call" | custom-call | tf_op jit(solution)/shard_map/pallas_call | solution.py:388
  (1 shorter events, 0.0 us)
Async XLA Ops:
  0.6 2.5 %copy-start = (bf16[1,1024,2048]{2,1,0:T(8,128)(2,1)S(1)}, bf16[1,1024,2048]{2,1,0:T(8,128)(2,1)}, u32[]{:S(2)}) copy-start(bf16[1,1024,2048]{2,1,0:T(8,128)(2,1)} %profile_at.1) | copy-start | bytes 12582916
  0.6 2.5 %copy-start.1 = (bf16[16,2048]{1,0:T(8,128)(2,1)S(1)}, bf16[16,2048]{1,0:T(8,128)(2,1)}, u32[]{:S(2)}) copy-start(bf16[16,2048]{1,0:T(8,128)(2,1)} %potential.1) | copy-start | bytes 196612

commit v2 on v1

--- a/solution.py
+++ b/solution.py
@@ -28,6 +28,10 @@
     return hop_square * (far[0] + share[0]), hop_square * (far[1] + share[1])
 
 
+def portions(valleys, blks, columns):
+    return [(slot, 0, columns) for slot in range(valleys * blks - 1)]
+
+
 def spread(energy, hopping, occupation, scalars):
     shape = scalars.shape[1:]
     scalars[0] = jnp.full(shape, energy[0])
@@ -40,16 +44,12 @@
     potential,
     profile_at,
     scalars,
-    mode_energy_at,
-    broadening_at,
-    self_left_at,
-    self_right_at,
-    charge_out,
-    density_out,
     mode_energy,
     broadening,
     self_left,
     self_right,
+    charge_out,
+    density_out,
     folded,
     small,
     terms,
@@ -61,9 +61,7 @@
     parts_in,
     send_sem,
     recv_sem,
-    send2_sem,
     recv2_sem,
-    small_sem,
 ):
     groups, valleys, blks = sizes
     slabs = potential.shape[0]
@@ -75,20 +73,6 @@
     me = lax.axis_index("slab")
     valley = lax.axis_index("valley")
     blk = lax.axis_index("blk")
-
-    small_loads = [
-        pltpu.make_async_copy(source, target, small_sem.at[slot])
-        for slot, (source, target) in enumerate(
-            [
-                (mode_energy_at, mode_energy),
-                (broadening_at, broadening),
-                (self_left_at, self_left),
-                (self_right_at, self_right),
-            ]
-        )
-    ]
-    for load in small_loads:
-        load.start()
 
     offsets = [(dv, db) for dv in range(1, valleys) for db in range(blks)]
     offsets += [(0, db) for db in range(1, blks)]
@@ -115,8 +99,6 @@
             row = first // LANES + j
             folded[pl.ds(row, slabs, stride=rows), :] = projected[:, j * LANES : (j + 1) * LANES]
 
-    for load in small_loads:
-        load.wait()
     hop_square = scalars[1]
     for j in range(rows):
         span = pl.ds(j * LANES, LANES)
@@ -179,37 +161,37 @@
 
     pl.semaphore_wait(barrier, groups - 1 + team - 1)
     inner = jnp.logical_and(me > 0, me < groups - 1)
-    planes = (pl.ds(0, 2), pl.ds(2, 4))
     routes = []
     for distance in range(groups - 1, 0, -1):
+        routes.append((me - distance, me + distance, groups - distance))
         routes.append((me + distance, me - distance, distance))
-        routes.append((me - distance, me + distance, groups - distance))
     sends = []
     for target, source, slot in routes:
-        copies = [
+        short, whole = [
             pltpu.make_async_remote_copy(
                 src_ref=own.at[plane],
                 dst_ref=others.at[slot, plane],
-                send_sem=send_sem.at[slot, which],
-                recv_sem=recv_sem.at[slot, which],
+                send_sem=send_sem.at[slot - 1],
+                recv_sem=recv_sem.at[slot - 1],
                 device_id={"slab": lax.rem(target + groups, groups)},
                 device_id_type=MESH,
             )
-            for which, plane in enumerate(planes)
+            for plane in (pl.ds(0, 2), pl.ds(0, 6))
         ]
         going = jnp.logical_and(target >= 0, target < groups)
         coming = jnp.logical_and(source >= 0, source < groups)
         full = jnp.logical_and(source > 0, source < groups - 1)
-        sends.append((copies, going, coming, full))
-    for copies, going, coming, full in sends:
-
-        @pl.when(going)
-        def _():
-            copies[0].start()
+        sends.append((short, whole, going, coming, full))
+    edge_here = jnp.logical_not(inner)
+    for short, whole, going, coming, full in sends:
+
+        @pl.when(jnp.logical_and(going, edge_here))
+        def _():
+            short.start()
 
         @pl.when(jnp.logical_and(going, inner))
         def _():
-            copies[1].start()
+            whole.start()
 
     segment = start(0)
     for s in range(slabs - 1):
@@ -224,15 +206,25 @@
         if s > 1:
             segment = grow(segment, s - 1)
 
-    for copies, going, coming, full in sends:
-
-        @pl.when(coming)
-        def _():
-            copies[0].wait_recv()
+    for short, whole, going, coming, full in sends:
+
+        @pl.when(jnp.logical_and(going, edge_here))
+        def _():
+            short.wait_send()
+
+        @pl.when(jnp.logical_and(going, inner))
+        def _():
+            whole.wait_send()
+
+    for short, whole, going, coming, full in sends:
+
+        @pl.when(jnp.logical_and(coming, jnp.logical_not(full)))
+        def _():
+            short.wait_recv()
 
         @pl.when(full)
         def _():
-            copies[1].wait_recv()
+            whole.wait_recv()
 
     def corners(ref, index):
         values = [ref[index, part] for part in range(6)]
@@ -271,39 +263,31 @@
         charge_out[0, :, pl.ds(j * LANES, LANES)] = terms[pl.ds(j, slabs, stride=rows), :]
     half = charge_out[0].astype(jnp.bfloat16)
 
-    def share(owner):
-        span = pl.ds(pl.multiple_of(owner * columns, columns), columns)
+    def share(owner, first, size):
+        span = pl.ds(pl.multiple_of(owner * columns + first, size), size)
         return jnp.dot(half, profile[:, span], preferred_element_type=jnp.float32)
 
     sends2 = []
-    for slot, (tv, tb) in enumerate(mates):
-        parts_own[slot] = share(tv * blks + tb)
+    for k, (slot, first, size) in enumerate(portions(valleys, blks, columns)):
+        tv, tb = mates[slot]
+        span = pl.ds(first, size)
+        parts_own[slot, :, span] = share(tv * blks + tb, first, size)
         send = pltpu.make_async_remote_copy(
-            src_ref=parts_own.at[slot],
-            dst_ref=parts_in.at[slot],
-            send_sem=send2_sem.at[slot],
-            recv_sem=recv2_sem.at[slot],
+            src_ref=parts_own.at[slot, :, span],
+            dst_ref=parts_in.at[slot, :, span],
+            send_sem=send_sem.at[k],
+            recv_sem=recv2_sem.at[k],
             device_id={"valley": tv, "blk": tb},
             device_id_type=MESH,
         )
         send.start()
-        sends2.append(send)
-    total = share(valley * blks + blk)
-    for slot in reversed(range(len(mates))):
-        sends2[slot].wait_recv()
-        total = total + parts_in[slot]
-    density_out[...] = total
-    for send in sends2:
+        sends2.append((send, slot, span))
+    density_out[...] = share(valley * blks + blk, 0, columns)
+    for send, slot, span in reversed(sends2):
+        send.wait_recv()
+        density_out[:, span] += parts_in[slot, :, span]
+    for send, slot, span in sends2:
         send.wait_send()
-    for copies, going, coming, full in sends:
-
-        @pl.when(going)
-        def _():
-            copies[0].wait_send()
-
-        @pl.when(jnp.logical_and(going, inner))
-        def _():
-            copies[1].wait_send()
 
 
 def drain(charge, density, charge_out, density_out, sem):
@@ -335,6 +319,7 @@
         modes, width = mode_density.shape[1:]
         rows = modes // LANES
         columns = width // team
+        pieces = len(portions(valleys, blks, columns))
         vmem = pl.BlockSpec(memory_space=pltpu.VMEM)
         smem = pl.BlockSpec(memory_space=pltpu.SMEM)
         hbm = pl.BlockSpec(memory_space=pltpu.HBM)
@@ -348,23 +333,15 @@
             ),
             compiler_params=pltpu.CompilerParams(vmem_limit_bytes=1024 * 1024),
         )(energy, hopping, occupation)
-        smalls = [
-            pltpu.with_memory_space_constraint(x, pltpu.HBM)
-            for x in (mode_energy, broadening, self_left, self_right)
-        ]
         outs = pl.pallas_call(
             functools.partial(kernel, sizes),
             out_shape=(
                 pltpu.VMEM((1, slabs, modes), jnp.float32),
                 pltpu.VMEM((slabs, columns), jnp.float32),
             ),
-            in_specs=[vmem, vmem, vmem, hbm, hbm, hbm, hbm],
+            in_specs=[vmem] * 7,
             out_specs=(vmem, vmem),
             scratch_shapes=[
-                pltpu.VMEM((1, modes), jnp.float32),
-                pltpu.VMEM((1, modes), jnp.float32),
-                pltpu.VMEM((1, 2, modes), jnp.float32),
-                pltpu.VMEM((1, 2, modes), jnp.float32),
                 pltpu.VMEM((slabs * rows, LANES), jnp.float32),
                 pltpu.VMEM((6, rows, LANES), jnp.float32),
                 pltpu.VMEM((slabs * rows, LANES), jnp.float32),
@@ -374,16 +351,14 @@
                 pltpu.VMEM((groups, 6, rows, LANES), jnp.float32),
                 pltpu.VMEM((max(team - 1, 1), slabs, columns), jnp.float32),
                 pltpu.VMEM((max(team - 1, 1), slabs, columns), jnp.float32),
-                pltpu.SemaphoreType.DMA((groups, 2)),
-                pltpu.SemaphoreType.DMA((groups, 2)),
-                pltpu.SemaphoreType.DMA((max(team - 1, 1),)),
-                pltpu.SemaphoreType.DMA((max(team - 1, 1),)),
-                pltpu.SemaphoreType.DMA((4,)),
+                pltpu.SemaphoreType.DMA((max(groups - 1, pieces, 1),)),
+                pltpu.SemaphoreType.DMA((max(groups - 1, 1),)),
+                pltpu.SemaphoreType.DMA((max(pieces, 1),)),
             ],
             compiler_params=pltpu.CompilerParams(
                 collective_id=0, has_side_effects=True, vmem_limit_bytes=8 * 1024 * 1024
             ),
-        )(potential, mode_density, scalars, *smalls)
+        )(potential, mode_density, scalars, mode_energy, broadening, self_left, self_right)
 
         return pl.pallas_call(
             drain,

time: 16.3 us -> 16.2 us (level)
  Pallas kernels: 12.9 us -> 12.7 us
    pallas_call x1, Pallas kernels: 12.3 us -> 12.1 us  [body(): pl.pallas_call(functools.partial(kernel, sizes), out_shape=(pltpu.VMEM((1...]
where the time goes in v2:
time: 16.2 us; the launch traced here: 16 us
  Pallas kernels  12.7 us (78%)
  between operations  3.26 us (20%)
    pallas_call x1, Pallas kernels, body(): pl.pallas_call(functools.partial(kernel, sizes), out_shape=(pltpu.VMEM((1...  12.1 us
    pallas_call x1, Pallas kernels, body(): pl.pallas_call(drain, out_shape=(jax.ShapeDtypeStruct((1, slabs, modes),...  0.66 us

profile of v2, /device:TPU:0, one launch (start us, length us, event | category | flops | bytes accessed | tf_op | source)
XLA Modules:
  0.0 16.0 jit_solution(9616708079314883176)
XLA Ops:
  0.6 0.0 copy-start.3
  0.6 0.0 copy-start.2
  0.7 0.0 copy-start.5
  0.7 0.0 copy-start.4
  0.7 0.0 copy-start
  0.7 0.0 copy-start.1
  3.2 0.0 copy-done.3
  3.2 0.0 copy-done.2
  3.2 0.0 copy-done.5
  3.2 0.0 copy-done.4
  3.3 0.0 copy-done
  3.3 0.0 copy-done.1
  3.3 12.1 %shard_map.105 = (f32[1,16,1024]{2,1,0:T(8,128)S(1)}, f32[16,512]{1,0:T(8,128)S(1)}) custom-call(bf16[16,2048]{1,0:T(8,128)(2,1)S(1)} %copy-done.1, bf16[1,1024,2048]{2,1,0:T(8,128)(2,1)S(1)} %copy-done, f32[3,8,128]{2,1,0:T(8,128)S(1)} %shard_map.104.scalars, f32[1,1024]{1,0:T(1,128)S(1)} %copy-done.4, f32[1,1024]{1,0:T(1,128)S(1)} %copy-done.5, ...), custom_call_target="tpu_custom_call" | custom-call | tf_op jit(solution)/shard_map/pallas_call | solution.py:336
  15.4 0.7 %shard_map.106 = (f32[1,16,1024]{2,1,0:T(8,128)}, f32[16,512]{1,0:T(8,128)}) custom-call(f32[1,16,1024]{2,1,0:T(8,128)S(1)} %get-tuple-element.4.charge, f32[16,512]{1,0:T(8,128)S(1)} %get-tuple-element.5.density), custom_call_target="tpu_custom_call" | custom-call | tf_op jit(solution)/shard_map/pallas_call | solution.py:363
  (1 shorter events, 0.0 us)
Async XLA Ops:
  0.6 2.6 %copy-start.3 = (f32[1,2,1024]{2,1,0:T(2,128)S(1)}, f32[1,2,1024]{2,1,0:T(2,128)}, u32[]{:S(2)}) copy-start(f32[1,2,1024]{2,1,0:T(2,128)} %self_right.1) | copy-start | bytes 24580
  0.6 2.6 %copy-start.2 = (f32[1,2,1024]{2,1,0:T(2,128)S(1)}, f32[1,2,1024]{2,1,0:T(2,128)}, u32[]{:S(2)}) copy-start(f32[1,2,1024]{2,1,0:T(2,128)} %self_left.1) | copy-start | bytes 24580
  0.7 2.6 %copy-start.5 = (f32[1,1024]{1,0:T(1,128)S(1)}, f32[1,1024]{1,0:T(1,128)}, u32[]{:S(2)}) copy-start(f32[1,1024]{1,0:T(1,128)} %broadening.1) | copy-start | bytes 12292
  0.7 2.6 %copy-start.4 = (f32[1,1024]{1,0:T(1,128)S(1)}, f32[1,1024]{1,0:T(1,128)}, u32[]{:S(2)}) copy-start(f32[1,1024]{1,0:T(1,128)} %mode_energy.1) | copy-start | bytes 12292
  0.7 2.6 %copy-start = (bf16[1,1024,2048]{2,1,0:T(8,128)(2,1)S(1)}, bf16[1,1024,2048]{2,1,0:T(8,128)(2,1)}, u32[]{:S(2)}) copy-start(bf16[1,1024,2048]{2,1,0:T(8,128)(2,1)} %profile_at.1) | copy-start | bytes 12582916
  0.7 2.6 %copy-start.1 = (bf16[16,2048]{1,0:T(8,128)(2,1)S(1)}, bf16[16,2048]{1,0:T(8,128)(2,1)}, u32[]{:S(2)}) copy-start(bf16[16,2048]{1,0:T(8,128)(2,1)} %potential.1) | copy-start | bytes 196612

commit v3 on v2

--- a/solution.py
+++ b/solution.py
@@ -44,12 +44,16 @@
     potential,
     profile_at,
     scalars,
+    mode_energy_at,
+    broadening_at,
+    self_left_at,
+    self_right_at,
+    charge_out,
+    density_out,
     mode_energy,
     broadening,
     self_left,
     self_right,
-    charge_out,
-    density_out,
     folded,
     small,
     terms,
@@ -62,6 +66,7 @@
     send_sem,
     recv_sem,
     recv2_sem,
+    prepared,
 ):
     groups, valleys, blks = sizes
     slabs = potential.shape[0]
@@ -73,6 +78,20 @@
     me = lax.axis_index("slab")
     valley = lax.axis_index("valley")
     blk = lax.axis_index("blk")
+
+    small_loads = [
+        pltpu.make_async_copy(source, target, send_sem.at[slot])
+        for slot, (source, target) in enumerate(
+            [
+                (mode_energy_at, mode_energy),
+                (broadening_at, broadening),
+                (self_left_at, self_left),
+                (self_right_at, self_right),
+            ]
+        )
+    ]
+    for load in small_loads:
+        load.start()
 
     offsets = [(dv, db) for dv in range(1, valleys) for db in range(blks)]
     offsets += [(0, db) for db in range(1, blks)]
@@ -99,6 +118,8 @@
             row = first // LANES + j
             folded[pl.ds(row, slabs, stride=rows), :] = projected[:, j * LANES : (j + 1) * LANES]
 
+    for load in small_loads:
+        load.wait()
     hop_square = scalars[1]
     for j in range(rows):
         span = pl.ds(j * LANES, LANES)
@@ -206,29 +227,48 @@
         if s > 1:
             segment = grow(segment, s - 1)
 
-    for short, whole, going, coming, full in sends:
-
-        @pl.when(jnp.logical_and(going, edge_here))
-        def _():
-            short.wait_send()
-
-        @pl.when(jnp.logical_and(going, inner))
-        def _():
-            whole.wait_send()
-
-    for short, whole, going, coming, full in sends:
-
-        @pl.when(jnp.logical_and(coming, jnp.logical_not(full)))
-        def _():
-            short.wait_recv()
-
-        @pl.when(full)
-        def _():
-            whole.wait_recv()
-
     def corners(ref, index):
         values = [ref[index, part] for part in range(6)]
         return values[0:2], values[2:4], values[4:6]
+
+    @pl.when(me == 0)
+    def _():
+        for s in range(slabs):
+            site = onsite(s)
+            a = begin
+            if s > 0:
+                near, cross, far = corners(heads, s - 1)
+                a = through(near, cross, far, hop_square, begin)
+            ahead = site[0] - a[0], site[1] - a[1]
+            slope = ahead
+            if s < slabs - 1:
+                near, cross, far = corners(tails, s)
+                ahead = ahead[0] - hop_square * far[0], ahead[1] - hop_square * far[1]
+                slope = times(ahead, near)
+                slope = slope[0] + hop_square * cross[0], slope[1] + hop_square * cross[1]
+            for part in range(2):
+                prepared[s, part] = ahead[part]
+                prepared[s, 2 + part] = slope[part]
+
+    for short, whole, going, coming, full in sends:
+
+        @pl.when(jnp.logical_and(going, edge_here))
+        def _():
+            short.wait_send()
+
+        @pl.when(jnp.logical_and(going, inner))
+        def _():
+            whole.wait_send()
+
+    for short, whole, going, coming, full in sends:
+
+        @pl.when(jnp.logical_and(coming, jnp.logical_not(full)))
+        def _():
+            short.wait_recv()
+
+        @pl.when(full)
+        def _():
+            whole.wait_recv()
 
     def go_right(k, term):
         near, cross, far = corners(others, me - k)
@@ -246,18 +286,35 @@
         right = lax.fori_loop(me + 2, groups, go_left, (others[edge, 0], others[edge, 1]))
 
     factor = scalars[2]
-    for s in range(slabs):
-        site = onsite(s)
-        a, b = left, right
-        if s > 0:
-            near, cross, far = corners(heads, s - 1)
-            a = through(near, cross, far, hop_square, left)
-        if s < slabs - 1:
-            near, cross, far = corners(tails, s)
-            b = through(near, cross, far, hop_square, right)
-        low_re = site[0] - a[0] - b[0]
-        low_im = site[1] - a[1] - b[1]
-        terms[pl.ds(s * rows, rows), :] = factor * low_im / (low_re * low_re + low_im * low_im)
+    @pl.when(me == 0)
+    def _():
+        for s in range(slabs):
+            ahead, slope = [[prepared[s, 2 * k + part] for part in range(2)] for k in range(2)]
+            if s < slabs - 1:
+                turn = times((tails[s, 0], tails[s, 1]), right)
+                drop = times(slope, right)
+                up_re, up_im = 1.0 - turn[0], -turn[1]
+                low_re, low_im = ahead[0] - drop[0], ahead[1] - drop[1]
+                value = up_re * low_im - up_im * low_re
+            else:
+                low_re, low_im = ahead[0] - right[0], ahead[1] - right[1]
+                value = low_im
+            terms[pl.ds(s * rows, rows), :] = factor * value / (low_re * low_re + low_im * low_im)
+
+    @pl.when(me != 0)
+    def _():
+        for s in range(slabs):
+            site = onsite(s)
+            a, b = left, right
+            if s > 0:
+                near, cross, far = corners(heads, s - 1)
+                a = through(near, cross, far, hop_square, left)
+            if s < slabs - 1:
+                near, cross, far = corners(tails, s)
+                b = through(near, cross, far, hop_square, right)
+            low_re = site[0] - a[0] - b[0]
+            low_im = site[1] - a[1] - b[1]
+            terms[pl.ds(s * rows, rows), :] = factor * low_im / (low_re * low_re + low_im * low_im)
 
     for j in range(rows):
         charge_out[0, :, pl.ds(j * LANES, LANES)] = terms[pl.ds(j, slabs, stride=rows), :]
@@ -333,15 +390,23 @@
             ),
             compiler_params=pltpu.CompilerParams(vmem_limit_bytes=1024 * 1024),
         )(energy, hopping, occupation)
+        smalls = [
+            pltpu.with_memory_space_constraint(x, pltpu.HBM)
+            for x in (mode_energy, broadening, self_left, self_right)
+        ]
         outs = pl.pallas_call(
             functools.partial(kernel, sizes),
             out_shape=(
                 pltpu.VMEM((1, slabs, modes), jnp.float32),
                 pltpu.VMEM((slabs, columns), jnp.float32),
             ),
-            in_specs=[vmem] * 7,
+            in_specs=[vmem] * 3 + [hbm] * 4,
             out_specs=(vmem, vmem),
             scratch_shapes=[
+                pltpu.VMEM((1, modes), jnp.float32),
+                pltpu.VMEM((1, modes), jnp.float32),
+                pltpu.VMEM((1, 2, modes), jnp.float32),
+                pltpu.VMEM((1, 2, modes), jnp.float32),
                 pltpu.VMEM((slabs * rows, LANES), jnp.float32),
                 pltpu.VMEM((6, rows, LANES), jnp.float32),
                 pltpu.VMEM((slabs * rows, LANES), jnp.float32),
@@ -351,14 +416,15 @@
                 pltpu.VMEM((groups, 6, rows, LANES), jnp.float32),
                 pltpu.VMEM((max(team - 1, 1), slabs, columns), jnp.float32),
                 pltpu.VMEM((max(team - 1, 1), slabs, columns), jnp.float32),
-                pltpu.SemaphoreType.DMA((max(groups - 1, pieces, 1),)),
+                pltpu.SemaphoreType.DMA((max(groups - 1, pieces, 4),)),
                 pltpu.SemaphoreType.DMA((max(groups - 1, 1),)),
                 pltpu.SemaphoreType.DMA((max(pieces, 1),)),
+                pltpu.VMEM((slabs, 4, rows, LANES), jnp.float32),
             ],
             compiler_params=pltpu.CompilerParams(
                 collective_id=0, has_side_effects=True, vmem_limit_bytes=8 * 1024 * 1024
             ),
-        )(potential, mode_density, scalars, mode_energy, broadening, self_left, self_right)
+        )(potential, mode_density, scalars, *smalls)
 
         return pl.pallas_call(
             drain,

time: 16.2 us -> 16 us (0.988)
  no operation moved by 1% of the time
where the time goes in v3:
time: 16 us; the launch traced here: 15.8 us
  Pallas kernels  12.7 us (79%)
  between operations  3.17 us (20%)
    pallas_call x1, Pallas kernels, body(): pl.pallas_call(functools.partial(kernel, sizes), out_shape=(pltpu.VMEM((1...  12 us
    pallas_call x1, Pallas kernels, body(): pl.pallas_call(drain, out_shape=(jax.ShapeDtypeStruct((1, slabs, modes),...  0.66 us

profile of v3, /device:TPU:0, one launch (start us, length us, event | category | flops | bytes accessed | tf_op | source)
XLA Modules:
  0.0 15.8 jit_solution(1135311499755375465)
XLA Ops:
  0.6 0.0 copy-start
  0.6 0.0 copy-start.1
  3.2 0.0 copy-done
  3.2 0.0 copy-done.1
  3.2 12.0 %shard_map.105 = (f32[1,16,1024]{2,1,0:T(8,128)S(1)}, f32[16,512]{1,0:T(8,128)S(1)}) custom-call(bf16[16,2048]{1,0:T(8,128)(2,1)S(1)} %copy-done.1, bf16[1,1024,2048]{2,1,0:T(8,128)(2,1)S(1)} %copy-done, f32[3,8,128]{2,1,0:T(8,128)S(1)} %shard_map.104.scalars, f32[1,1024]{1,0:T(1,128)} %mode_energy_at.1, f32[1,1024]{1,0:T(1,128)} %broadening_at.1, ...), custom_call_target="tpu_custom_call" | custom-call | tf_op jit(solution)/shard_map/pallas_call | solution.py:397
  15.2 0.7 %shard_map.106 = (f32[1,16,1024]{2,1,0:T(8,128)}, f32[16,512]{1,0:T(8,128)}) custom-call(f32[1,16,1024]{2,1,0:T(8,128)S(1)} %get-tuple-element.4.charge, f32[16,512]{1,0:T(8,128)S(1)} %get-tuple-element.5.density), custom_call_target="tpu_custom_call" | custom-call | tf_op jit(solution)/shard_map/pallas_call | solution.py:429
  (1 shorter events, 0.0 us)
Async XLA Ops:
  0.6 2.5 %copy-start = (bf16[1,1024,2048]{2,1,0:T(8,128)(2,1)S(1)}, bf16[1,1024,2048]{2,1,0:T(8,128)(2,1)}, u32[]{:S(2)}) copy-start(bf16[1,1024,2048]{2,1,0:T(8,128)(2,1)} %profile_at.1) | copy-start | bytes 12582916
  0.6 2.5 %copy-start.1 = (bf16[16,2048]{1,0:T(8,128)(2,1)S(1)}, bf16[16,2048]{1,0:T(8,128)(2,1)}, u32[]{:S(2)}) copy-start(bf16[16,2048]{1,0:T(8,128)(2,1)} %potential.1) | copy-start | bytes 196612

commit v4 on v3

--- a/solution.py
+++ b/solution.py
@@ -10,7 +10,7 @@
 
 MESH = pl.DeviceIdType.MESH
 LANES = 128
-PIECE = 256
+PIECE = 512
 
 
 def times(x, y):
@@ -67,6 +67,7 @@
     recv_sem,
     recv2_sem,
     prepared,
+    half,
 ):
     groups, valleys, blks = sizes
     slabs = potential.shape[0]
@@ -285,6 +286,21 @@
         left = lax.fori_loop(1, me, go_right, (others[me, 0], others[me, 1]))
         right = lax.fori_loop(me + 2, groups, go_left, (others[edge, 0], others[edge, 1]))
 
+    def share(owner, first, size):
+        span = pl.ds(pl.multiple_of(owner * columns + first, size), size)
+        return jnp.dot(half[...], profile[:, span], preferred_element_type=jnp.float32)
+
+    orders = portions(valleys, blks, columns)
+
+    def contribute():
+        for j in range(rows):
+            charge_out[0, :, pl.ds(j * LANES, LANES)] = terms[pl.ds(j, slabs, stride=rows), :]
+        half[...] = charge_out[0].astype(jnp.bfloat16)
+        if orders:
+            slot, first, size = orders[0]
+            tv, tb = mates[slot]
+            parts_own[slot, :, pl.ds(first, size)] = share(tv * blks + tb, first, size)
+
     factor = scalars[2]
     @pl.when(me == 0)
     def _():
@@ -300,6 +316,7 @@
                 low_re, low_im = ahead[0] - right[0], ahead[1] - right[1]
                 value = low_im
             terms[pl.ds(s * rows, rows), :] = factor * value / (low_re * low_re + low_im * low_im)
+        contribute()
 
     @pl.when(me != 0)
     def _():
@@ -315,20 +332,14 @@
             low_re = site[0] - a[0] - b[0]
             low_im = site[1] - a[1] - b[1]
             terms[pl.ds(s * rows, rows), :] = factor * low_im / (low_re * low_re + low_im * low_im)
-
-    for j in range(rows):
-        charge_out[0, :, pl.ds(j * LANES, LANES)] = terms[pl.ds(j, slabs, stride=rows), :]
-    half = charge_out[0].astype(jnp.bfloat16)
-
-    def share(owner, first, size):
-        span = pl.ds(pl.multiple_of(owner * columns + first, size), size)
-        return jnp.dot(half, profile[:, span], preferred_element_type=jnp.float32)
+        contribute()
 
     sends2 = []
-    for k, (slot, first, size) in enumerate(portions(valleys, blks, columns)):
+    for k, (slot, first, size) in enumerate(orders):
         tv, tb = mates[slot]
         span = pl.ds(first, size)
-        parts_own[slot, :, span] = share(tv * blks + tb, first, size)
+        if k > 0:
+            parts_own[slot, :, span] = share(tv * blks + tb, first, size)
         send = pltpu.make_async_remote_copy(
             src_ref=parts_own.at[slot, :, span],
             dst_ref=parts_in.at[slot, :, span],
@@ -420,6 +431,7 @@
                 pltpu.SemaphoreType.DMA((max(groups - 1, 1),)),
                 pltpu.SemaphoreType.DMA((max(pieces, 1),)),
                 pltpu.VMEM((slabs, 4, rows, LANES), jnp.float32),
+                pltpu.VMEM((slabs, modes), jnp.bfloat16),
             ],
             compiler_params=pltpu.CompilerParams(
                 collective_id=0, has_side_effects=True, vmem_limit_bytes=8 * 1024 * 1024

time: 16 us -> 16 us (level)
  no operation moved by 1% of the time
where the time goes in v4:
time: 16 us; the launch traced here: 15.8 us
  Pallas kernels  12.7 us (79%)
  between operations  3.17 us (20%)
    pallas_call x1, Pallas kernels, body(): pl.pallas_call(functools.partial(kernel, sizes), out_shape=(pltpu.VMEM((1...  12 us
    pallas_call x1, Pallas kernels, body(): pl.pallas_call(drain, out_shape=(jax.ShapeDtypeStruct((1, slabs, modes),...  0.66 us

profile of v4, /device:TPU:0, one launch (start us, length us, event | category | flops | bytes accessed | tf_op | source)
XLA Modules:
  0.0 15.8 jit_solution(15522341647710421652)
XLA Ops:
  0.6 0.0 copy-start
  0.6 0.0 copy-start.1
  3.2 0.0 copy-done
  3.2 0.0 copy-done.1
  3.2 12.0 %shard_map.105 = (f32[1,16,1024]{2,1,0:T(8,128)S(1)}, f32[16,512]{1,0:T(8,128)S(1)}) custom-call(bf16[16,2048]{1,0:T(8,128)(2,1)S(1)} %copy-done.1, bf16[1,1024,2048]{2,1,0:T(8,128)(2,1)S(1)} %copy-done, f32[3,8,128]{2,1,0:T(8,128)S(1)} %shard_map.104.scalars, f32[1,1024]{1,0:T(1,128)} %mode_energy_at.1, f32[1,1024]{1,0:T(1,128)} %broadening_at.1, ...), custom_call_target="tpu_custom_call" | custom-call | tf_op jit(solution)/shard_map/pallas_call | solution.py:408
  15.2 0.7 %shard_map.106 = (f32[1,16,1024]{2,1,0:T(8,128)}, f32[16,512]{1,0:T(8,128)}) custom-call(f32[1,16,1024]{2,1,0:T(8,128)S(1)} %get-tuple-element.4.charge, f32[16,512]{1,0:T(8,128)S(1)} %get-tuple-element.5.density), custom_call_target="tpu_custom_call" | custom-call | tf_op jit(solution)/shard_map/pallas_call | solution.py:441
  (1 shorter events, 0.0 us)
Async XLA Ops:
  0.6 2.5 %copy-start = (bf16[1,1024,2048]{2,1,0:T(8,128)(2,1)S(1)}, bf16[1,1024,2048]{2,1,0:T(8,128)(2,1)}, u32[]{:S(2)}) copy-start(bf16[1,1024,2048]{2,1,0:T(8,128)(2,1)} %profile_at.1) | copy-start | bytes 12582916
  0.6 2.5 %copy-start.1 = (bf16[16,2048]{1,0:T(8,128)(2,1)S(1)}, bf16[16,2048]{1,0:T(8,128)(2,1)}, u32[]{:S(2)}) copy-start(bf16[16,2048]{1,0:T(8,128)(2,1)} %potential.1) | copy-start | bytes 196612

commit v5 on v3

--- a/solution.py
+++ b/solution.py
@@ -10,7 +10,7 @@
 
 MESH = pl.DeviceIdType.MESH
 LANES = 128
-PIECE = 256
+PIECE = 512
 
 
 def times(x, y):

time: 16 us -> 16 us (level)
  no operation moved by 1% of the time
where the time goes in v5:
time: 16 us; the launch traced here: 15.8 us
  Pallas kernels  12.7 us (79%)
  between operations  3.17 us (20%)
    pallas_call x1, Pallas kernels, body(): pl.pallas_call(functools.partial(kernel, sizes), out_shape=(pltpu.VMEM((1...  12 us
    pallas_call x1, Pallas kernels, body(): pl.pallas_call(drain, out_shape=(jax.ShapeDtypeStruct((1, slabs, modes),...  0.66 us

profile of v5, /device:TPU:0, one launch (start us, length us, event | category | flops | bytes accessed | tf_op | source)
XLA Modules:
  0.0 15.8 jit_solution(1135311499755375465)
XLA Ops:
  0.6 0.0 copy-start
  0.6 0.0 copy-start.1
  3.2 0.0 copy-done
  3.2 0.0 copy-done.1
  3.2 12.0 %shard_map.105 = (f32[1,16,1024]{2,1,0:T(8,128)S(1)}, f32[16,512]{1,0:T(8,128)S(1)}) custom-call(bf16[16,2048]{1,0:T(8,128)(2,1)S(1)} %copy-done.1, bf16[1,1024,2048]{2,1,0:T(8,128)(2,1)S(1)} %copy-done, f32[3,8,128]{2,1,0:T(8,128)S(1)} %shard_map.104.scalars, f32[1,1024]{1,0:T(1,128)} %mode_energy_at.1, f32[1,1024]{1,0:T(1,128)} %broadening_at.1, ...), custom_call_target="tpu_custom_call" | custom-call | tf_op jit(solution)/shard_map/pallas_call | solution.py:397
  15.2 0.7 %shard_map.106 = (f32[1,16,1024]{2,1,0:T(8,128)}, f32[16,512]{1,0:T(8,128)}) custom-call(f32[1,16,1024]{2,1,0:T(8,128)S(1)} %get-tuple-element.4.charge, f32[16,512]{1,0:T(8,128)S(1)} %get-tuple-element.5.density), custom_call_target="tpu_custom_call" | custom-call | tf_op jit(solution)/shard_map/pallas_call | solution.py:429
  (1 shorter events, 0.0 us)
Async XLA Ops:
  0.6 2.5 %copy-start = (bf16[1,1024,2048]{2,1,0:T(8,128)(2,1)S(1)}, bf16[1,1024,2048]{2,1,0:T(8,128)(2,1)}, u32[]{:S(2)}) copy-start(bf16[1,1024,2048]{2,1,0:T(8,128)(2,1)} %profile_at.1) | copy-start | bytes 12582916
  0.6 2.5 %copy-start.1 = (bf16[16,2048]{1,0:T(8,128)(2,1)S(1)}, bf16[16,2048]{1,0:T(8,128)(2,1)}, u32[]{:S(2)}) copy-start(bf16[16,2048]{1,0:T(8,128)(2,1)} %potential.1) | copy-start | bytes 196612
